TPU v7x, 128 devices: a whole 4x4x4 slice. The times are simulated.
128 devices in a mesh: task: 8 (over x_hi, z), dp: 16 (over x_lo, y, core).
Axes of the slice: x: 4 (x_hi: 2, x_lo: 2; x = x_hi * 2 + x_lo), y: 4, z: 4, core: 2. Of those that a mesh axis runs over, the one named last changes fastest.
Arguments:
- tokens_in: bfloat16 [131072, 4096], P(('task', 'dp')), may hold values from -45 to 45
- query_cotangent: bfloat16 [131072, 2048], P(('task', 'dp')), may hold values from -23040 to 23040
- task_index: int32 [131072], P(('task', 'dp')), may hold values from 0 to 15, as said below
- loss_weights: int32 [16], replicated, may hold values from 1 to 4
- master: float32 [4096, 2048], P(('task', 'dp')), may hold values from -6 to 6
- moment_first: float32 [4096, 2048], P(('task', 'dp')), may hold values from -6 to 6
- moment_second: float32 [4096, 2048], P(('task', 'dp')), may hold values from 0.05 to 5
Outputs:
- new_master: float32 [4096, 2048], P(('task', 'dp'))
- new_first: float32 [4096, 2048], P(('task', 'dp'))
- new_second: float32 [4096, 2048], P(('task', 'dp'))
Inputs may be any that keep to these rules, and one draw needn't show every extreme that they name: `task_index`: the first 16 tokens name each task once.
All inputs are finite; a program needn't handle non-finite values.
Results may differ from a plain program's by a relative error of at most 0.00042.
Values may be sent and summed in bfloat16 or wider, within the bound.
A program may use at most 192 MiB of HBM per device.

v0:
```python
import jax
import jax.numpy as jnp
from jax import lax
from jax.sharding import Mesh
from jax.sharding import PartitionSpec as P

D = 4096
QW = 2048
TASK_DP = ("task_0", "task_1", "dp_0", "dp_1", "dp_2")
TASK = ("task_0", "task_1")
DP = ("dp_0", "dp_1", "dp_2")


beta_one = 0.9
beta_two = 0.95
adam_eps = 1e-08
step_rate = 0.01
decay_rate = 0.1
corr_one = 1.0 - 0.9**10
corr_two = 1.0 - 0.95**10


def over_axes(value, axes):
    for axis in axes:
        value = lax.psum(value, axis)
    return value


def split_up(value, dim, size):
    shape = value.shape
    blocks = value.reshape(*shape[:dim], size, shape[dim] // size, *shape[dim + 1 :])
    return jnp.moveaxis(blocks, dim, 0)


def summed_on_arrival(value, axis, dim):
    blocks = split_up(value, dim, lax.axis_size(axis))
    arrived = lax.all_to_all(blocks, axis, split_axis=0, concat_axis=0, tiled=True)
    return arrived.sum(axis=0)


def shards(
    tokens_in, query_cotangent, task_index, loss_weights, master, moment_first, moment_second
):
    labels = lax.iota(jnp.int32, loss_weights.shape[0])
    member = task_index[:, None] == labels[None, :]
    local_counts = jnp.sum(member.astype(jnp.int32), axis=0)
    counts = over_axes(local_counts, TASK_DP)
    task_scale = loss_weights.astype(jnp.float32) / counts.astype(jnp.float32)
    token_scale = jnp.sum(jnp.where(member, task_scale[None, :], jnp.float32(0.0)), axis=1)
    weighted = (query_cotangent.astype(jnp.float32) * token_scale[:, None]).astype(jnp.bfloat16)
    out_rows = master.shape[0]
    feature_count = weighted.shape[1]
    group_count = lax.axis_size(TASK)
    lane_count = lax.axis_size(DP)
    arranged = tokens_in.reshape(tokens_in.shape[0], group_count, lane_count, out_rows)
    group_rows = group_count * out_rows
    products = jnp.einsum("ntdr,nq->dtrq", arranged, weighted, preferred_element_type=jnp.float32)
    partial_value = lax.psum_scatter(
        products.reshape(lax.axis_size(DP) * group_rows, feature_count),
        DP,
        scatter_dimension=0,
        tiled=True,
    )
    gradient = summed_on_arrival(partial_value, TASK, 0)
    square_sum = over_axes(jnp.sum(gradient * gradient), TASK_DP)
    root_mean = jnp.sqrt(square_sum / (D * QW))
    factor = 1.0 / jnp.maximum(root_mean, 1.0)
    clipped = gradient * factor
    new_first = beta_one * moment_first + (1.0 - beta_one) * clipped
    new_second = beta_two * moment_second + (1.0 - beta_two) * clipped * clipped
    direction = new_first / corr_one / (jnp.sqrt(new_second / corr_two) + adam_eps)
    new_master = master - step_rate * (direction + decay_rate * master)
    return (new_master, new_first, new_second)


def solution(mesh):
    finer = Mesh(mesh.devices.reshape(2, 4, 2, 4, 2), ("task_0", "task_1", "dp_0", "dp_1", "dp_2"))
    in_specs = (
        P(TASK_DP, None),
        P(TASK_DP, None),
        P(TASK_DP),
        P(),
        P(TASK_DP, None),
        P(TASK_DP, None),
        P(TASK_DP, None),
    )
    out_specs = (P(TASK_DP, None), P(TASK_DP, None), P(TASK_DP, None))
    return jax.shard_map(
        shards, mesh=finer, in_specs=in_specs, out_specs=out_specs, check_vma=False
    )
```

profile of v0, /device:TPU:0, one launch (start us, length us, event | category | flops | bytes accessed | tf_op | source)
XLA Modules:
  0.0 348.0 jit_solution(1351179126321543253)
XLA Ops:
  7.2 0.0 reduce-scatter.2.cloned.1.call-start
  7.2 0.8 convert_reduce_fusion
  8.0 5.8 %psum.70 = s32[16]{0:T(128)S(1)} all-reduce(s32[16]{0:T(128)S(1)} %convert_reduce_fusion), channel_id=1, replica_groups=mesh['task_0'=2,'task_1'=4,'dp_0'=2,'dp_1'=4,'dp_2'=2] {'task_0'}, use_global_device_ids=true, to_apply=%region_1.0 | all-reduce | flops 16 | bytes 128 | tf_op jit(solution)/shard_map/psum | solution.py:25
  13.8 9.8 %psum.71 = s32[16]{0:T(128)S(1)} all-reduce(s32[16]{0:T(128)S(1)} %psum.70), channel_id=1, replica_groups=mesh['task_0'=2,'task_1'=4,'dp_0'=2,'dp_1'=4,'dp_2'=2] {'task_1'}, use_global_device_ids=true, to_apply=%region_2.0 | all-reduce | flops 16 | bytes 128 | tf_op jit(solution)/shard_map/psum | solution.py:25
  23.6 4.3 %psum.72 = s32[16]{0:T(128)S(1)} all-reduce(s32[16]{0:T(128)S(1)} %psum.71), channel_id=1, replica_groups=mesh['task_0'=2,'task_1'=4,'dp_0'=2,'dp_1'=4,'dp_2'=2] {'dp_0'}, use_global_device_ids=true, to_apply=%region_3.0 | all-reduce | flops 16 | bytes 128 | tf_op jit(solution)/shard_map/psum | solution.py:25
  27.9 9.0 %psum.73 = s32[16]{0:T(128)S(1)} all-reduce(s32[16]{0:T(128)S(1)} %psum.72), channel_id=1, replica_groups=mesh['task_0'=2,'task_1'=4,'dp_0'=2,'dp_1'=4,'dp_2'=2] {'dp_1'}, use_global_device_ids=true, to_apply=%region_4.0 | all-reduce | flops 16 | bytes 128 | tf_op jit(solution)/shard_map/psum | solution.py:25
  36.9 1.8 psum.74
  38.8 0.7 convert_divide_fusion
  39.4 0.8 select_reduce_fusion
  40.2 26.0 %fusion = f32[2048,4096]{0,1} fusion(bf16[1024,4096]{1,0:T(8,128)(2,1)} %param.7, bf16[1024,2048]{1,0:T(8,128)(2,1)} %param.8, f32[1024]{0:T(1024)S(1)} %select_reduce_fusion), kind=kOutput, calls=%fused_computation.1 | convolution fusion | flops 17186160640 | bytes 46141440
  66.2 23.0 %copy.14 = f32[16,8,32,2048]{3,2,1,0:T(8,128)} copy(f32[16,8,32,2048]{3,2,0,1:T(8,128)} %bitcast.10) | data formatting | bytes 67108864 | tf_op jit(solution)/shard_map/ntdr,nq->dtrq/transpose | solution.py:57
  89.2 0.0 copy-start
  89.2 0.0 copy-start.1
  89.2 0.0 copy-start.2
  89.2 0.0 reduce-scatter.2.cloned.1.call-update
  89.2 180.0 %reduce-scatter.2.cloned.1.call-done = f32[256,2048]{1,0:T(8,128)} async-done(((f32[4096,2048]{1,0:T(8,128)}), f32[256,2048]{1,0:T(8,128)}) %reduce-scatter.2.cloned.1.call-update) | async-done | bytes 2097168 | tf_op jit(solution)/shard_map/reduce_scatter | solution.py:58
  269.2 33.8 %all_to_all.5 = f32[8,32,2048]{2,1,0:T(8,128)S(1)} all-to-all(f32[8,32,2048]{2,1,0:T(8,128)} %bitcast.11), channel_id=1, replica_groups=mesh['task_0'=2,'task_1'=4,'dp_0'=2,'dp_1'=4,'dp_2'=2] {'task_0','task_1'}, dimensions={0} | all-to-all | bytes 4194304 | tf_op jit(solution)/shard_map/all_to_all | solution.py:37
  303.0 0.1 reduce_sum.38
  303.1 0.7 multiply_reduce_fusion
  303.8 7.0 %psum.75 = f32[]{:T(128)} all-reduce(f32[]{:T(128)} %multiply_reduce_fusion), channel_id=1, replica_groups=mesh['task_0'=2,'task_1'=4,'dp_0'=2,'dp_1'=4,'dp_2'=2] {'task_0'}, use_global_device_ids=true, to_apply=%region_10.11 | all-reduce | flops 1 | bytes 8 | tf_op jit(solution)/shard_map/psum | solution.py:25
  310.8 9.2 %psum.76 = f32[]{:T(128)} all-reduce(f32[]{:T(128)} %psum.75), channel_id=1, replica_groups=mesh['task_0'=2,'task_1'=4,'dp_0'=2,'dp_1'=4,'dp_2'=2] {'task_1'}, use_global_device_ids=true, to_apply=%region_11.12 | all-reduce | flops 1 | bytes 8 | tf_op jit(solution)/shard_map/psum | solution.py:25
  320.0 5.5 %psum.77 = f32[]{:T(128)} all-reduce(f32[]{:T(128)} %psum.76), channel_id=1, replica_groups=mesh['task_0'=2,'task_1'=4,'dp_0'=2,'dp_1'=4,'dp_2'=2] {'dp_0'}, use_global_device_ids=true, to_apply=%region_12.13 | all-reduce | flops 1 | bytes 8 | tf_op jit(solution)/shard_map/psum | solution.py:25
  325.5 10.8 %psum.78 = f32[]{:T(128)} all-reduce(f32[]{:T(128)} %psum.77), channel_id=1, replica_groups=mesh['task_0'=2,'task_1'=4,'dp_0'=2,'dp_1'=4,'dp_2'=2] {'dp_1'}, use_global_device_ids=true, to_apply=%region_13.14 | all-reduce | flops 1 | bytes 8 | tf_op jit(solution)/shard_map/psum | solution.py:25
  336.3 3.1 psum.79
  340.1 0.0 copy-done
  340.1 0.0 copy-done.1
  340.1 0.0 copy-done.2
  340.1 1.0 multiply_subtract_fusion
Async XLA Ops:
  7.2 262.0 %reduce-scatter.2.cloned.1.call-start = ((), (), s32[]{:S(2)}) async-start(), calls=%async_computation.2 | async-start | bytes 35651584 | tf_op jit(solution)/shard_map/reduce_scatter | solution.py:58
  89.2 250.9 %copy-start = (f32[32,2048]{1,0:T(8,128)S(1)}, f32[32,2048]{1,0:T(8,128)}, u32[]{:S(2)}) copy-start(f32[32,2048]{1,0:T(8,128)} %param.11) | copy-start | bytes 786436
  89.2 250.9 %copy-start.1 = (f32[32,2048]{1,0:T(8,128)S(1)}, f32[32,2048]{1,0:T(8,128)}, u32[]{:S(2)}) copy-start(f32[32,2048]{1,0:T(8,128)} %param.12) | copy-start | bytes 786436
  89.2 250.9 %copy-start.2 = (f32[32,2048]{1,0:T(8,128)S(1)}, f32[32,2048]{1,0:T(8,128)}, u32[]{:S(2)}) copy-start(f32[32,2048]{1,0:T(8,128)} %param.13) | copy-start | bytes 786436
Sparse Core Ops, SparseCore 0:
  89.3 179.8 reduce-scatter.1
where the time goes:
time: 350 us; the launch traced here: 348 us
  waiting for transfers between devices  180 us (51%)
  blocking collectives  100 us (29%)
  matrix products  26 us (7%)
  local copies, waits for them, and re-layouts  23 us (7%)
  between operations  14.8 us (4%)
  other arithmetic  4.03 us (1%)
    reduce_scatter x1, waiting for transfers between devices, shards(): lax.psum_scatter(products.reshape(lax.axis_size(DP) * group_rows, feature...  180 us
    psum x10, blocking collectives, over_axes(): value = lax.psum(value, axis)  66.3 us
    all_to_all x1, blocking collectives, summed_on_arrival(): lax.all_to_all(blocks, axis, split_axis=0, concat_axis=0, tiled=True)  33.8 us
    unnamed x1, matrix products  26 us
    transpose x1, local copies, waits for them, and re-layouts, shards(): jnp.einsum('ntdr,nq->dtrq', arranged, weighted, preferred_element_type=jn...  23 us
  transfers between devices with their start and end apart: 1, of which 1 were waited for; matrix products, arithmetic and copies ran while one was open for 0% of the time, Pallas kernels for 0%

commit v1 on v0

v1 whole, which is shorter than its diff:
```python
import jax
import jax.numpy as jnp
from jax import lax
from jax.experimental import pallas as pl
from jax.experimental.pallas import tpu as pltpu
from jax.sharding import Mesh
from jax.sharding import PartitionSpec as P

D = 4096
QW = 2048
TASKS = 16
AXES = ("task_0", "task_1", "dp_0", "dp_1", "dp_2")
MESH = pl.DeviceIdType.MESH

beta_one = 0.9
beta_two = 0.95
adam_eps = 1e-08
step_rate = 0.01
decay_rate = 0.1
corr_one = 1.0 - 0.9**10
corr_two = 1.0 - 0.95**10

TOK = 1024
HALF = QW // 2
C0, W0 = 0, 384
C1, W1 = 384, 384
C2, W2 = 768, 256
LAG = 3
DX = (2, 2, 0, 1, 2, 3, 2, 1, 1, 0, 3, 1, 3, 0, 3, 0)
DZ = (2, 0, 2, 2, 1, 2, 3, 1, 0, 1, 1, 3, 0, 3, 3, 0)
TOP = 32766.0


def pick(i, table):
    out = jnp.int32(table[0])
    for j in range(1, len(table)):
        out = jnp.where(i == j, jnp.int32(table[j]), out)
    return out


def tiles(rows, width):
    return (rows // 16) * (width // 128)


def encode(src, r0, rows, c0, width, msg):
    nc = width // 128

    def largest(t, m):
        for j in range(nc):
            a = jnp.abs(src[pl.ds(r0 + t * 16, 16), pl.ds(c0 + j * 128, 128)])
            m = jnp.maximum(m, jnp.maximum(a[:8], a[8:]))
        return m

    m = lax.fori_loop(0, rows // 16, largest, jnp.zeros((8, 128), jnp.float32), unroll=2)
    e = jnp.ceil(jnp.log2(jnp.maximum(m, 1e-30)) + 0.001)
    inv = jnp.exp2(-e) * TOP
    inv = jnp.concatenate([inv, inv], axis=0)

    def put(t, carry):
        for j in range(nc):
            v = src[pl.ds(r0 + t * 16, 16), pl.ds(c0 + j * 128, 128)]
            msg[t * nc + j] = jnp.round(v * inv).astype(jnp.int32).astype(jnp.int16)
        return carry

    lax.fori_loop(0, rows // 16, put, 0, unroll=2)
    msg[tiles(rows, width)] = jnp.concatenate([e, e], axis=0).astype(jnp.int32).astype(jnp.int16)


def decode_add(dst, r0, rows, c0, width, msg):
    nc = width // 128
    e = msg[tiles(rows, width)].astype(jnp.int32).astype(jnp.float32)
    scale = jnp.exp2(e) * (1.0 / TOP)

    def add(t, carry):
        for j in range(nc):
            at = (pl.ds(r0 + t * 16, 16), pl.ds(c0 + j * 128, 128))
            dst[at] = dst[at] + msg[t * nc + j].astype(jnp.int32).astype(jnp.float32) * scale
        return carry

    lax.fori_loop(0, rows // 16, add, 0, unroll=2)


def copy_rows(dst, dr0, src, sr0, rows, c0, width):
    def put(t, carry):
        for j in range(width // 128):
            dst[pl.ds(dr0 + t * 16, 16), pl.ds(j * 128, 128)] = src[
                pl.ds(sr0 + t * 16, 16), pl.ds(c0 + j * 128, 128)
            ]
        return carry

    lax.fori_loop(0, rows // 16, put, 0, unroll=2)


def kernel(
    tok_hbm, cot_hbm, idx_hbm, lw_smem, grad_ref, clip_ref,
    tok, w, idx, tsc, acc,
    own0, own1, own2, hold1,
    sA0, rA0, sB0, rB0,
    sA2, rA2, sB2, rB2,
    sA1, rA1, sB1, rB1,
    s2A, r2A, s2B, r2B, s2A2, r2A2, s2B2, r2B2,
    s3A, r3A, s3B, r3B, s3A2, r3A2, s3B2, r3B2,
    cnt1, cnt2, nrm1, nrm2, fin, finr,
    loc_sem, tok_s, tok_r, in_s, in_r,
    one_s, one_r, two_s, two_r, none_s, none_r, ntwo_s, ntwo_r,
    a0_s, a0_r, b0_s, b0_r, a1_s, a1_r, b1_s, b1_r, a2_s, a2_r, b2_s, b2_r,
    p2_s, p2_r, p3_s, p3_r, f_s, f_r,
):
    xh = lax.axis_index("task_0")
    Z = lax.axis_index("task_1")
    xl = lax.axis_index("dp_0")
    Y = lax.axis_index("dp_1")
    C = lax.axis_index("dp_2")
    X = xh * 2 + xl

    def dev(x, y, z, c):
        return (lax.div(x, 2), z, lax.rem(x, 2), y, c)

    def rem4(v):
        return lax.rem(v, 4)

    me = (X, Y, Z, C)
    xp, xm = dev(rem4(X + 1), Y, Z, C), dev(rem4(X + 3), Y, Z, C)
    yp, ym = dev(X, rem4(Y + 1), Z, C), dev(X, rem4(Y + 3), Z, C)
    zp, zm = dev(X, Y, rem4(Z + 1), C), dev(X, Y, rem4(Z + 3), C)
    partner = dev(X, Y, Z, 1 - C)

    def near(k):
        p = lax.rem(Y * 2 + C + k, 8)
        return dev(X, lax.div(p, 2), Z, lax.rem(p, 2))

    def far(k):
        p = lax.rem(X * 4 + Z + k, 16)
        return dev(lax.div(p, 4), Y, lax.rem(p, 4), C)

    def remote(src, dst, ssem, rsem, to):
        return pltpu.make_async_remote_copy(
            src_ref=src, dst_ref=dst, send_sem=ssem, recv_sem=rsem, device_id=to, device_id_type=MESH
        )

    def row0(x, z):
        return pl.multiple_of(lax.div(x, 2) * 2048 + z * 512 + lax.rem(x, 2) * 256, 256)

    def group(i):
        x = rem4(X + pick(i, DX))
        z = rem4(Z + pick(i, DZ))
        return x, z

    my_cols = pl.ds(pl.multiple_of(C * HALF, HALF), HALF)
    other_cols = pl.ds(pl.multiple_of((1 - C) * HALF, HALF), HALF)
    cp_idx = pltpu.make_async_copy(idx_hbm, idx.at[0], loc_sem.at[0])
    cp_cot = pltpu.make_async_copy(cot_hbm.at[:, my_cols], w.at[0], loc_sem.at[1])
    cp_idx.start()
    cp_cot.start()

    barrier = pltpu.get_barrier_semaphore()
    for k in range(1, 8):
        pl.semaphore_signal(barrier, inc=1, device_id=near(k), device_id_type=MESH)
    for k in range(1, 16):
        pl.semaphore_signal(barrier, inc=1, device_id=far(k), device_id_type=MESH)

    def local_tok(i):
        x, z = group(i)
        cols = pl.ds(row0(x, z), 256)
        return pltpu.make_async_copy(tok_hbm.at[:, cols], tok.at[0, :, cols], loc_sem.at[2 + i])

    def remote_tok(i):
        x, z = group(i)
        cols = pl.ds(row0(x, z), 256)
        return remote(tok_hbm.at[:, cols], tok.at[1, :, cols], tok_s.at[i], tok_r.at[i], partner)

    cp_idx.wait()
    own_idx = idx[0]
    here = Y * 2 + C
    for k in range(TASKS):
        cnt1[pl.ds(here, 1), pl.ds(k, 1), :] = jnp.sum(
            (own_idx == k).astype(jnp.int32), axis=0, keepdims=True
        )[None]
    pl.semaphore_wait(barrier, 22)

    def exchange(slots, at, count, to, ssem, rsem):
        copies = []
        for k in range(1, count):
            c = remote(slots.at[at], slots.at[at], ssem.at[k], rsem.at[k], to(k))
            c.start()
            copies.append(c)
        return copies

    def arrived(slots, at, count, to, ssem, rsem):
        for k in range(1, count):
            src = lax.rem(at + count - k, count)
            remote(slots.at[src], slots.at[src], ssem.at[k], rsem.at[k], to(k)).wait_recv()

    first = exchange(cnt1, here, 8, near, one_s, one_r)
    in_cot = remote(cot_hbm.at[:, other_cols], w.at[1], in_s.at[0], in_r.at[0], partner)
    in_idx = remote(idx_hbm, idx.at[1], in_s.at[1], in_r.at[1], partner)
    in_idx.start()
    in_cot.start()

    def start_tok(i, carry):
        local_tok(i).start()
        remote_tok(i).start()
        return carry

    lax.fori_loop(0, 16, start_tok, 0)

    arrived(cnt1, here, 8, near, one_s, one_r)
    plane = X * 4 + Z
    total = cnt1[0]
    for k in range(1, 8):
        total = total + cnt1[k]
    cnt2[plane] = total
    second = exchange(cnt2, plane, 16, far, two_s, two_r)
    arrived(cnt2, plane, 16, far, two_s, two_r)
    total = cnt2[0]
    for k in range(1, 16):
        total = total + cnt2[k]
    counts = jnp.sum(total, axis=1, keepdims=True)
    counts = jnp.broadcast_to(counts, (TASKS, 128)).astype(jnp.float32)

    in_idx.wait_recv()
    for s in range(2):
        ids = idx[s]
        scale = jnp.zeros((8, 128), jnp.float32)
        for k in range(TASKS):
            weight = lw_smem[k].astype(jnp.float32) / counts[k : k + 1, :]
            scale = jnp.where(ids == k, jnp.broadcast_to(weight, (8, 128)), scale)
        tsc[s] = scale
    cp_cot.wait()
    in_cot.wait_recv()

    for s in range(2):

        def weigh(b, carry):
            row = tsc[s, pl.ds(b, 1), :]
            mat = jnp.broadcast_to(row, (128, 128)).T
            rows = pl.ds(pl.multiple_of(b * 128, 128), 128)
            for j in range(HALF // 128):
                cols = pl.ds(j * 128, 128)
                w[s, rows, cols] = (w[s, rows, cols].astype(jnp.float32) * mat).astype(jnp.bfloat16)
            return carry

        lax.fori_loop(0, 8, weigh, 0)

    def A0(z, side):
        return remote(sA0.at[z, side], rA0.at[z, side], a0_s.at[z, side], a0_r.at[z, side], (xp, xm)[side])

    def B0(z, side):
        return remote(sB0.at[z, side], rB0.at[z, side], b0_s.at[z, side], b0_r.at[z, side], (xp, xm)[side])

    def A2(x, side):
        return remote(sA2.at[x, side], rA2.at[x, side], a2_s.at[x, side], a2_r.at[x, side], (zp, zm)[side])

    def B2(x, side):
        return remote(sB2.at[x, side], rB2.at[x, side], b2_s.at[x, side], b2_r.at[x, side], (zp, zm)[side])

    def A1(g, side):
        return remote(sA1.at[g, side], rA1.at[g, side], a1_s.at[g, side], a1_r.at[g, side], (yp, ym)[side])

    def B1(g, side):
        return remote(sB1.at[g, side], rB1.at[g, side], b1_s.at[g, side], b1_r.at[g, side], (yp, ym)[side])

    def first_phase(d, n, c0, width, own, A, B, sA, rA, sB):
        @pl.when(d == 2)
        def _():
            for side in range(2):
                encode(acc, 128 * side, 128, c0, width, sA.at[n, side])
                A(n, side).start()

        for side in range(2):

            @pl.when(d == 1 + 2 * side)
            def _():
                A(n, side).wait_recv()
                decode_add(acc, 128 * side, 128, c0, width, rA.at[n, side])
                encode(acc, 0, 256, c0, width, sB.at[n, side])
                B(n, side).start()

        @pl.when(d == 0)
        def _():
            copy_rows(own.at[n], 0, acc, 0, 256, c0, width)

    def late(i):
        x, z = group(i)
        g = x * 4 + z
        for side in range(2):
            A1(g, side).wait_recv()
            decode_add(hold1.at[g, side], 32 * side, 32, 0, W1, rA1.at[g, side])
            encode(hold1.at[g, side], 0, 64, 0, W1, sB1.at[g, side])
            B1(g, side).start()

    def step(i, carry):
        x, z = group(i)
        g = x * 4 + z
        cols = pl.ds(row0(x, z), 256)
        local_tok(i).wait()
        remote_tok(i).wait_recv()
        dims = (((0,), (0,)), ((), ()))
        acc[...] = lax.dot_general(
            tok[0, :, cols], w[0], dims, preferred_element_type=jnp.float32
        ) + lax.dot_general(tok[1, :, cols], w[1], dims, preferred_element_type=jnp.float32)
        dx = rem4(x + 4 - X)
        dz = rem4(z + 4 - Z)
        first_phase(dx, z, C0, W0, own0, A0, B0, sA0, rA0, sB0)
        y2 = pl.multiple_of(rem4(Y + 2) * 64, 64)
        for side in range(2):
            encode(acc, y2 + 32 * side, 32, C1, W1, sA1.at[g, side])
            A1(g, side).start()
        copy_rows(hold1.at[g, 0], 0, acc, pl.multiple_of(rem4(Y + 1) * 64, 64), 64, C1, W1)
        copy_rows(hold1.at[g, 1], 0, acc, pl.multiple_of(rem4(Y + 3) * 64, 64), 64, C1, W1)
        copy_rows(own1.at[z], pl.multiple_of(x * 64, 64), acc, pl.multiple_of(Y * 64, 64), 64, C1, W1)
        first_phase(dz, x, C2, W2, own2, A2, B2, sA2, rA2, sB2)

        @pl.when(i >= LAG)
        def _():
            late(i - LAG)

        return carry

    lax.fori_loop(0, 16, step, 0)

    def late_step(i, carry):
        late(i)
        return carry

    lax.fori_loop(16 - LAG, 16, late_step, 0)

    def ring(sA, rA, sB, rB, ss, rs, n, plus, minus):
        def A(side):
            return remote(sA.at[side], rA.at[side], ss.at[n, side], rs.at[n, side], (plus, minus)[side])

        def B(side):
            return remote(sB.at[side], rB.at[side], ss.at[n, 2 + side], rs.at[n, 2 + side], (plus, minus)[side])

        return A, B

    second_rings = (
        (own0, W0, Z, s2A.at[0], r2A.at[0], s2B.at[0], r2B.at[0], zp, zm),
        (own1, W1, Z, s2A.at[1], r2A.at[1], s2B.at[1], r2B.at[1], zp, zm),
        (own2, W2, X, s2A2, r2A2, s2B2, r2B2, xp, xm),
    )

    def gather(n, m):
        if n == 0:
            for side in range(2):
                B0(m, side).wait_recv()
                decode_add(own0.at[m], 0, 256, 0, W0, rB0.at[m, side])
        elif n == 2:
            for side in range(2):
                B2(m, side).wait_recv()
                decode_add(own2.at[m], 0, 256, 0, W2, rB2.at[m, side])
        else:

            def one(x, carry):
                g = x * 4 + m
                for side in range(2):
                    B1(g, side).wait_recv()
                    decode_add(own1.at[m], pl.multiple_of(x * 64, 64), 64, 0, W1, rB1.at[g, side])
                return carry

            lax.fori_loop(0, 4, one, 0)

    for n, (own, width, at, sA, rA, sB, rB, plus, minus) in enumerate(second_rings):
        A, B = ring(sA, rA, sB, rB, p2_s, p2_r, n, plus, minus)
        m = rem4(at + 2)
        gather(n, m)
        for side in range(2):
            encode(own.at[m], 128 * side, 128, 0, width, sA.at[side])
            A(side).start()
    for n, (own, width, at, sA, rA, sB, rB, plus, minus) in enumerate(second_rings):
        A, B = ring(sA, rA, sB, rB, p2_s, p2_r, n, plus, minus)
        for side in range(2):
            m = rem4(at + 1 + 2 * side)
            gather(n, m)
            A(side).wait_recv()
            decode_add(own.at[m], 128 * side, 128, 0, width, rA.at[side])
            encode(own.at[m], 0, 256, 0, width, sB.at[side])
            B(side).start()
    for n in range(3):
        gather(n, second_rings[n][2])
    for n, (own, width, at, sA, rA, sB, rB, plus, minus) in enumerate(second_rings):
        A, B = ring(sA, rA, sB, rB, p2_s, p2_r, n, plus, minus)
        for side in range(2):
            B(side).wait_recv()
            decode_add(own.at[at], 0, 256, 0, width, rB.at[side])

    third_rings = (
        (own0.at[Z], W0, Y, s3A.at[0], r3A.at[0], s3B.at[0], r3B.at[0], yp, ym),
        (own1.at[Z], W1, X, s3A.at[1], r3A.at[1], s3B.at[1], r3B.at[1], xp, xm),
        (own2.at[X], W2, Y, s3A2, r3A2, s3B2, r3B2, yp, ym),
    )
    for n, (own, width, at, sA, rA, sB, rB, plus, minus) in enumerate(third_rings):
        A, B = ring(sA, rA, sB, rB, p3_s, p3_r, n, plus, minus)
        r = pl.multiple_of(rem4(at + 2) * 64, 64)
        for side in range(2):
            encode(own, r + 32 * side, 32, 0, width, sA.at[side])
            A(side).start()
    for n, (own, width, at, sA, rA, sB, rB, plus, minus) in enumerate(third_rings):
        A, B = ring(sA, rA, sB, rB, p3_s, p3_r, n, plus, minus)
        for side in range(2):
            r = pl.multiple_of(rem4(at + 1 + 2 * side) * 64, 64)
            A(side).wait_recv()
            decode_add(own, r + 32 * side, 32, 0, width, rA.at[side])
            encode(own, r, 64, 0, width, sB.at[side])
            B(side).start()
    col = 0
    square = jnp.zeros((8, 128), jnp.float32)
    for n, (own, width, at, sA, rA, sB, rB, plus, minus) in enumerate(third_rings):
        A, B = ring(sA, rA, sB, rB, p3_s, p3_r, n, plus, minus)
        r = pl.multiple_of(at * 64, 64)
        for side in range(2):
            B(side).wait_recv()
            decode_add(own, r, 64, 0, width, rB.at[side])
        for t in range(8):
            for j in range(width // 128):
                v = own[pl.ds(r + t * 8, 8), pl.ds(j * 128, 128)]
                fin[pl.ds(t * 8, 8), pl.ds(col + j * 128, 128)] = v
                square = square + v * v
        col += width

    nrm1[here] = square
    third = exchange(nrm1, here, 8, near, none_s, none_r)
    theirs = pl.ds(pl.multiple_of((1 - C) * 32, 32), 32)
    mine = pl.ds(pl.multiple_of(C * 32, 32), 32)
    swap = remote(fin.at[theirs], finr, f_s, f_r, partner)
    swap.start()
    grad_ref[:, my_cols] = fin[mine, :]
    arrived(nrm1, here, 8, near, none_s, none_r)
    square = nrm1[0]
    for k in range(1, 8):
        square = square + nrm1[k]
    nrm2[plane] = square
    fourth = exchange(nrm2, plane, 16, far, ntwo_s, ntwo_r)
    swap.wait_recv()
    grad_ref[:, other_cols] = finr[...]

    def sent(z, carry):
        for side in range(2):
            A0(z, side).wait_send()
            B0(z, side).wait_send()
            A2(z, side).wait_send()
            B2(z, side).wait_send()
        return carry

    lax.fori_loop(0, 4, sent, 0)

    def sent1(g, carry):
        for side in range(2):
            A1(g, side).wait_send()
            B1(g, side).wait_send()
        remote_tok(g).wait_send()
        return carry

    lax.fori_loop(0, 16, sent1, 0)
    for rings, ss, rs in ((second_rings, p2_s, p2_r), (third_rings, p3_s, p3_r)):
        for n, (own, width, at, sA, rA, sB, rB, plus, minus) in enumerate(rings):
            A, B = ring(sA, rA, sB, rB, ss, rs, n, plus, minus)
            for side in range(2):
                A(side).wait_send()
                B(side).wait_send()
    in_cot.wait_send()
    in_idx.wait_send()
    swap.wait_send()
    for c in first + second + third + fourth:
        c.wait_send()

    arrived(nrm2, plane, 16, far, ntwo_s, ntwo_r)
    square = nrm2[0]
    for k in range(1, 16):
        square = square + nrm2[k]
    clip_ref[...] = jnp.broadcast_to(jnp.sum(square, keepdims=True), (8, 128))


def shards(tokens_in, query_cotangent, task_index, loss_weights, master, moment_first, moment_second):
    i16 = jnp.int16

    def msgs(lead, rows, width):
        return pltpu.VMEM((*lead, tiles(rows, width) + 1, 16, 128), i16)

    f32 = jnp.float32
    dma = pltpu.SemaphoreType.DMA
    scratch = [
        pltpu.VMEM((2, TOK, D), jnp.bfloat16),
        pltpu.VMEM((2, TOK, HALF), jnp.bfloat16),
        pltpu.VMEM((2, 8, 128), jnp.int32),
        pltpu.VMEM((2, 8, 128), f32),
        pltpu.VMEM((256, HALF), f32),
        pltpu.VMEM((4, 256, W0), f32),
        pltpu.VMEM((4, 256, W1), f32),
        pltpu.VMEM((4, 256, W2), f32),
        pltpu.VMEM((16, 2, 64, W1), f32),
        msgs((4, 2), 128, W0), msgs((4, 2), 128, W0), msgs((4, 2), 256, W0), msgs((4, 2), 256, W0),
        msgs((4, 2), 128, W2), msgs((4, 2), 128, W2), msgs((4, 2), 256, W2), msgs((4, 2), 256, W2),
        msgs((16, 2), 32, W1), msgs((16, 2), 32, W1), msgs((16, 2), 64, W1), msgs((16, 2), 64, W1),
        msgs((2, 2), 128, W0), msgs((2, 2), 128, W0), msgs((2, 2), 256, W0), msgs((2, 2), 256, W0),
        msgs((2,), 128, W2), msgs((2,), 128, W2), msgs((2,), 256, W2), msgs((2,), 256, W2),
        msgs((2, 2), 32, W0), msgs((2, 2), 32, W0), msgs((2, 2), 64, W0), msgs((2, 2), 64, W0),
        msgs((2,), 32, W2), msgs((2,), 32, W2), msgs((2,), 64, W2), msgs((2,), 64, W2),
        pltpu.VMEM((8, TASKS, 128), jnp.int32),
        pltpu.VMEM((16, TASKS, 128), jnp.int32),
        pltpu.VMEM((8, 8, 128), f32),
        pltpu.VMEM((16, 8, 128), f32),
        pltpu.VMEM((64, HALF), f32),
        pltpu.VMEM((32, HALF), f32),
        dma((18,)), dma((16,)), dma((16,)), dma((2,)), dma((2,)),
        dma((8,)), dma((8,)), dma((16,)), dma((16,)), dma((8,)), dma((8,)), dma((16,)), dma((16,)),
        dma((4, 2)), dma((4, 2)), dma((4, 2)), dma((4, 2)),
        dma((16, 2)), dma((16, 2)), dma((16, 2)), dma((16, 2)),
        dma((4, 2)), dma((4, 2)), dma((4, 2)), dma((4, 2)),
        dma((3, 4)), dma((3, 4)), dma((3, 4)), dma((3, 4)),
        dma(()), dma(()),
    ]
    hbm = pl.BlockSpec(memory_space=pl.ANY)
    vmem = pl.BlockSpec(memory_space=pltpu.VMEM)
    gradient, square = pl.pallas_call(
        kernel,
        out_shape=(
            jax.ShapeDtypeStruct((32, QW), f32),
            jax.ShapeDtypeStruct((8, 128), f32),
        ),
        in_specs=[hbm, hbm, hbm, pl.BlockSpec(memory_space=pltpu.SMEM)],
        out_specs=(vmem, vmem),
        scratch_shapes=scratch,
        compiler_params=pltpu.CompilerParams(
            collective_id=0, has_side_effects=True, vmem_limit_bytes=63 * 1024 * 1024
        ),
    )(tokens_in, query_cotangent, task_index.reshape(8, 128), loss_weights)
    root_mean = jnp.sqrt(square[0, 0] / (D * QW))
    factor = 1.0 / jnp.maximum(root_mean, 1.0)
    clipped = gradient * factor
    new_first = beta_one * moment_first + (1.0 - beta_one) * clipped
    new_second = beta_two * moment_second + (1.0 - beta_two) * clipped * clipped
    direction = new_first / corr_one / (jnp.sqrt(new_second / corr_two) + adam_eps)
    new_master = master - step_rate * (direction + decay_rate * master)
    return (new_master, new_first, new_second)


def solution(mesh):
    finer = Mesh(mesh.devices.reshape(2, 4, 2, 4, 2), AXES)
    rows = P(AXES, None)
    in_specs = (rows, rows, P(AXES), P(), rows, rows, rows)
    return jax.shard_map(
        shards, mesh=finer, in_specs=in_specs, out_specs=(rows, rows, rows), check_vma=False
    )
```

time: 350 us -> 95.3 us (0.27)
  waiting for transfers between devices: 180 us -> 0 us
  blocking collectives: 100 us -> 0 us
  Pallas kernels: 0 us -> 90.1 us
  matrix products: 26 us -> 0 us
  local copies, waits for them, and re-layouts: 23 us -> 1.2 us
  between operations: 14.8 us -> 1.42 us
    reduce_scatter x1 -> x0, waiting for transfers between devices: 180 us -> none  [shards(): lax.psum_scatter(products.reshape(lax.axis_size(DP) * group_rows, feature...]
    pallas_call x0 -> x1, Pallas kernels: none -> 90.1 us  [shards(): pl.pallas_call(kernel, out_shape=(jax.ShapeDtypeStruct((32, QW), f32), ja...]
    psum x10 -> x0, blocking collectives: 66.3 us -> none  [over_axes(): value = lax.psum(value, axis)]
    all_to_all x1 -> x0, blocking collectives: 33.8 us -> none  [summed_on_arrival(): lax.all_to_all(blocks, axis, split_axis=0, concat_axis=0, tiled=True)]
    unnamed x1 -> x0, matrix products: 26 us -> none
    transpose x1 -> x0, local copies, waits for them, and re-layouts: 23 us -> none  [shards(): jnp.einsum('ntdr,nq->dtrq', arranged, weighted, preferred_element_type=jn...]
  transfers between devices with their start and end apart: 1 -> 0, of which waited for: 1 -> 0; matrix products, arithmetic and copies ran while one was open for 0% -> 0% of each run, Pallas kernels for 0% -> 0%
where the time goes in v1:
time: 95.3 us; the launch traced here: 94.7 us
  Pallas kernels  90.1 us (95%)
  other arithmetic  1.95 us (2%)
  between operations  1.42 us (1%)
  local copies, waits for them, and re-layouts  1.2 us (1%)
    pallas_call x1, Pallas kernels, shards(): pl.pallas_call(kernel, out_shape=(jax.ShapeDtypeStruct((32, QW), f32), ja...  90.1 us
    sub x1, other arithmetic, shards(): new_master = master - step_rate * (direction + decay_rate * master)  1.95 us

profile of v1, /device:TPU:0, one launch (start us, length us, event | category | flops | bytes accessed | tf_op | source)
XLA Modules:
  0.0 94.7 jit_solution(7127814348346277296)
XLA Ops:
  0.6 0.0 copy-start.2
  0.6 0.0 copy-start.1
  0.7 0.0 copy-start
  0.7 90.1 %shard_map.94 = (f32[32,2048]{1,0:T(8,128)}, f32[8,128]{1,0:T(8,128)}) custom-call(bf16[1024,4096]{1,0:T(8,128)(2,1)} %tok_hbm.1, bf16[1024,2048]{1,0:T(8,128)(2,1)} %cot_hbm.1, s32[8,128]{1,0:T(8,128)} %bitcast.2, s32[16]{0:T(128)} %lw_smem.1), custom_call_target="tpu_custom_call" | custom-call | tf_op jit(solution)/shard_map/pallas_call | solution.py:515
  90.8 1.2 %slice.3 = f32[1,1]{1,0:T(1,128)} slice(f32[8,128]{1,0:T(8,128)} %get-tuple-element.6), slice={[0:1], [0:1]} | slice | bytes 8 | tf_op jit(solution)/shard_map/slice | solution.py:528
  92.7 0.0 copy-done.2
  92.7 0.0 copy-done.1
  92.8 0.0 copy-done
  92.8 2.0 %multiply_subtract_fusion = (f32[32,2048]{1,0:T(8,128)}, f32[32,2048]{1,0:T(8,128)}, f32[32,2048]{1,0:T(8,128)}) fusion(f32[32,2048]{1,0:T(8,128)S(1)} %copy-done, f32[32,2048]{1,0:T(8,128)} %get-tuple-element.5, f32[]{:T(128)} %bitcast.1, f32[32,2048]{1,0:T(8,128)S(1)} %copy-done.1, f32[32,2048]{1,0:T(8,128)S(1)} %copy-done.2), kind=kLoop, calls=%fused_computation.2 | loop fusion | flops 1048576 | bytes 1835012 | tf_op jit(solution)/shard_map/sub | solution.py:534
Async XLA Ops:
  0.6 92.1 %copy-start.2 = (f32[32,2048]{1,0:T(8,128)S(1)}, f32[32,2048]{1,0:T(8,128)}, u32[]{:S(2)}) copy-start(f32[32,2048]{1,0:T(8,128)} %param.13) | copy-start | bytes 786436
  0.6 92.1 %copy-start.1 = (f32[32,2048]{1,0:T(8,128)S(1)}, f32[32,2048]{1,0:T(8,128)}, u32[]{:S(2)}) copy-start(f32[32,2048]{1,0:T(8,128)} %param.12) | copy-start | bytes 786436
  0.7 92.1 %copy-start = (f32[32,2048]{1,0:T(8,128)S(1)}, f32[32,2048]{1,0:T(8,128)}, u32[]{:S(2)}) copy-start(f32[32,2048]{1,0:T(8,128)} %param.11) | copy-start | bytes 786436

commit v2 on v0

v2 whole, which is shorter than its diff:
```python
import jax
import jax.numpy as jnp
from jax import lax
from jax.experimental import pallas as pl
from jax.experimental.pallas import tpu as pltpu
from jax.sharding import Mesh
from jax.sharding import PartitionSpec as P

D = 4096
QW = 2048
TASKS = 16
AXES = ("task_0", "task_1", "dp_0", "dp_1", "dp_2")
MESH = pl.DeviceIdType.MESH

beta_one = 0.9
beta_two = 0.95
adam_eps = 1e-08
step_rate = 0.01
decay_rate = 0.1
corr_one = 1.0 - 0.9**10
corr_two = 1.0 - 0.95**10

TOK = 1024
HALF = QW // 2
C0, W0 = 0, 384
C1, W1 = 384, 384
C2, W2 = 768, 256
LAG_B = 3
LAG_SUM = 6
SLOTS = 8
ORDER = (2, 1, 3, 0)
FETCH_X = (0, 1, 0, 2, 0, 3, 0, 1, 2, 1, 3, 1, 2, 3, 2, 3)
FETCH_Z = (0, 0, 1, 0, 2, 0, 3, 1, 1, 2, 1, 3, 2, 2, 3, 3)
NEED = (1, 2, 2, 2, 0, 1, 2, 2, 0, 0, 1, 2, 0, 0, 0, 1)
HAVE = (0, 1, 3, 5, 7, 7, 8, 10, 12, 12, 12, 13, 15, 15, 15, 15)
TOP = 32766.0


def pick(i, table):
    out = jnp.int32(table[0])
    for j in range(1, len(table)):
        out = jnp.where(i == j, jnp.int32(table[j]), out)
    return out


def tiles(rows, width):
    return (rows // 16) * (width // 128)


def encode(src, r0, rows, c0, width, msg):
    nc = width // 128
    unroll = min(8, rows // 16)

    def largest(t, ms):
        out = []
        for j in range(nc):
            a = jnp.abs(src[pl.ds(r0 + t * 16, 16), pl.ds(c0 + j * 128, 128)])
            out.append(jnp.maximum(ms[2 * j], a[:8]))
            out.append(jnp.maximum(ms[2 * j + 1], a[8:]))
        return tuple(out)

    zero = jnp.zeros((8, 128), jnp.float32)
    ms = lax.fori_loop(0, rows // 16, largest, (zero,) * (2 * nc), unroll=unroll)
    m = ms[0]
    for other in ms[1:]:
        m = jnp.maximum(m, other)
    e = jnp.ceil(jnp.log2(jnp.maximum(m, 1e-30)) + 0.001)
    inv = jnp.exp2(-e) * TOP
    inv = jnp.concatenate([inv, inv], axis=0)

    def put(t, carry):
        for j in range(nc):
            v = src[pl.ds(r0 + t * 16, 16), pl.ds(c0 + j * 128, 128)]
            msg[t * nc + j] = jnp.round(v * inv).astype(jnp.int32).astype(jnp.int16)
        return carry

    lax.fori_loop(0, rows // 16, put, 0, unroll=unroll)
    msg[tiles(rows, width)] = jnp.concatenate([e, e], axis=0).astype(jnp.int32).astype(jnp.int16)


def decode_sum(dst, dr0, dc0, src, sr0, sc0, rows, width, msgs):
    nc = width // 128
    scales = []
    for msg in msgs:
        e = msg[tiles(rows, width)].astype(jnp.int32).astype(jnp.float32)
        scales.append(jnp.exp2(e) * (1.0 / TOP))

    def add(t, carry):
        for j in range(nc):
            v = src[pl.ds(sr0 + t * 16, 16), pl.ds(sc0 + j * 128, 128)]
            for msg, scale in zip(msgs, scales):
                v = v + msg[t * nc + j].astype(jnp.int32).astype(jnp.float32) * scale
            dst[pl.ds(dr0 + t * 16, 16), pl.ds(dc0 + j * 128, 128)] = v
        return carry

    lax.fori_loop(0, rows // 16, add, 0, unroll=min(8, rows // 16))


def kernel(
    tok_hbm, cot_hbm, idx_hbm, lw_hbm, grad_ref,
    lw, tok, w, idx, tsc, acc,
    own0, own1, own2,
    sA0, rA0, sB0, rB0,
    sA2, rA2, sB2, rB2,
    sA1, rA1, sB1, rB1,
    s2A, r2A, s2B, r2B, s2A2, r2A2, s2B2, r2B2,
    s3, r3, s32, r32,
    cnt1, cnt2, nrm1, nrm2, fin, finr,
    loc_sem, tok_s, tok_r, in_s, in_r,
    one_s, one_r, two_s, two_r, none_s, none_r, ntwo_s, ntwo_r,
    a0_s, a0_r, b0_s, b0_r, a1_s, a1_r, b1_s, b1_r, a2_s, a2_r, b2_s, b2_r,
    p2a_s, p2a_r, p2b_s, p2b_r, p3_s, p3_r, f_s, f_r,
):
    xh = lax.axis_index("task_0")
    Z = lax.axis_index("task_1")
    xl = lax.axis_index("dp_0")
    Y = lax.axis_index("dp_1")
    C = lax.axis_index("dp_2")
    X = xh * 2 + xl

    def dev(x, y, z, c):
        return (lax.div(x, 2), z, lax.rem(x, 2), y, c)

    def rem4(v):
        return lax.rem(v, 4)

    me = (X, Y, Z, C)
    xp, xm = dev(rem4(X + 1), Y, Z, C), dev(rem4(X + 3), Y, Z, C)
    yp, ym = dev(X, rem4(Y + 1), Z, C), dev(X, rem4(Y + 3), Z, C)
    zp, zm = dev(X, Y, rem4(Z + 1), C), dev(X, Y, rem4(Z + 3), C)
    partner = dev(X, Y, Z, 1 - C)

    def near(k):
        p = lax.rem(Y * 2 + C + k, 8)
        return dev(X, lax.div(p, 2), Z, lax.rem(p, 2))

    def far(k):
        p = lax.rem(X * 4 + Z + k, 16)
        return dev(lax.div(p, 4), Y, lax.rem(p, 4), C)

    def remote(src, dst, ssem, rsem, to):
        return pltpu.make_async_remote_copy(
            src_ref=src, dst_ref=dst, send_sem=ssem, recv_sem=rsem, device_id=to, device_id_type=MESH
        )

    def row0(x, z):
        return pl.multiple_of(lax.div(x, 2) * 2048 + z * 512 + lax.rem(x, 2) * 256, 256)

    def place(p, q):
        return rem4(X + pick(p, ORDER)), rem4(Z + pick(q, ORDER))

    my_cols = pl.ds(pl.multiple_of(C * HALF, HALF), HALF)
    other_cols = pl.ds(pl.multiple_of((1 - C) * HALF, HALF), HALF)
    cp_idx = pltpu.make_async_copy(idx_hbm, idx.at[0], loc_sem.at[0])
    cp_cot = pltpu.make_async_copy(cot_hbm.at[:, my_cols], w.at[0], loc_sem.at[1])
    cp_lw = pltpu.make_async_copy(lw_hbm, lw, loc_sem.at[2])
    cp_idx.start()
    cp_lw.start()
    cp_cot.start()

    barrier = pltpu.get_barrier_semaphore()
    for k in range(1, 8):
        pl.semaphore_signal(barrier, inc=1, device_id=near(k), device_id_type=MESH)
    for k in range(1, 16):
        pl.semaphore_signal(barrier, inc=1, device_id=far(k), device_id_type=MESH)

    def local_tok(i):
        x, z = place(pick(i, FETCH_X), pick(i, FETCH_Z))
        cols = pl.ds(row0(x, z), 256)
        return pltpu.make_async_copy(tok_hbm.at[:, cols], tok.at[0, :, cols], loc_sem.at[3 + i])

    def remote_tok(i):
        x, z = place(pick(i, FETCH_X), pick(i, FETCH_Z))
        cols = pl.ds(row0(x, z), 256)
        return remote(tok_hbm.at[:, cols], tok.at[1, :, cols], tok_s, tok_r.at[i], partner)

    cp_idx.wait()
    own_idx = idx[0]
    here = Y * 2 + C
    lane = lax.broadcasted_iota(jnp.int32, (1, 128), 1)
    member = jnp.zeros((1, 128), jnp.int32)
    for k in range(TASKS):
        count = jnp.sum(jnp.sum((own_idx == k).astype(jnp.int32), axis=0, keepdims=True), axis=1, keepdims=True)
        member = jnp.where(lane == k, jnp.broadcast_to(count, (1, 128)), member)
    cnt1[here] = member
    pl.semaphore_wait(barrier, 22)

    def exchange(slots, at, count, to, ssem, rsem):
        for k in range(1, count):
            remote(slots.at[at], slots.at[at], ssem, rsem, to(k)).start()

    def everything(slots, count, ssem, rsem):
        some = slots.at[pl.ds(0, count - 1)]
        return remote(some, some, ssem, rsem, partner)

    def total_of(slots, count):
        total = slots[0]
        for k in range(1, count):
            total = total + slots[k]
        return total

    exchange(cnt1, here, 8, near, one_s, one_r)
    in_cot = remote(cot_hbm.at[:, other_cols], w.at[1], in_s.at[0], in_r.at[0], partner)
    in_idx = remote(idx_hbm, idx.at[1], in_s.at[1], in_r.at[1], partner)
    in_idx.start()
    in_cot.start()

    def start_tok(i, carry):
        local_tok(i).start()
        remote_tok(i).start()
        return carry

    lax.fori_loop(0, 16, start_tok, 0)

    everything(cnt1, 8, one_s, one_r).wait_recv()
    plane = X * 4 + Z
    cnt2[plane] = total_of(cnt1, 8)
    exchange(cnt2, plane, 16, far, two_s, two_r)
    everything(cnt2, 16, two_s, two_r).wait_recv()
    counts = jnp.broadcast_to(total_of(cnt2, 16), (TASKS, 128))
    diagonal = lax.broadcasted_iota(jnp.int32, (TASKS, 128), 0) == lax.broadcasted_iota(
        jnp.int32, (TASKS, 128), 1
    )
    counts = jnp.sum(jnp.where(diagonal, counts, 0), axis=1, keepdims=True)
    counts = jnp.broadcast_to(counts, (TASKS, 128)).astype(jnp.float32)
    cp_lw.wait()

    in_idx.wait_recv()
    for s in range(2):
        ids = idx[s]
        scale = jnp.zeros((8, 128), jnp.float32)
        for k in range(TASKS):
            weight = lw[k].astype(jnp.float32) / counts[k : k + 1, :]
            scale = jnp.where(ids == k, jnp.broadcast_to(weight, (8, 128)), scale)
        tsc[s] = scale
    cp_cot.wait()
    in_cot.wait_recv()

    for s in range(2):

        def weigh(b, carry):
            row = tsc[s, pl.ds(b, 1), :]
            mat = jnp.broadcast_to(row, (128, 128)).T
            rows = pl.ds(pl.multiple_of(b * 128, 128), 128)
            for j in range(HALF // 128):
                cols = pl.ds(j * 128, 128)
                w[s, rows, cols] = (w[s, rows, cols].astype(jnp.float32) * mat).astype(jnp.bfloat16)
            return carry

        lax.fori_loop(0, 8, weigh, 0)

    def message(S, R, ss, rs, ways):
        def at(n, side):
            return remote(S.at[n, side], R.at[n, side], ss, rs.at[n, side], ways[side])

        return at

    def halves(S, R, ss, rs, ways):
        def at(n, side, half):
            return remote(S.at[n, side, half], R.at[n, side, half], ss, rs.at[n], ways[side])

        return at

    def both(S, R, ss, rs, n):
        return remote(S.at[n], R.at[n], ss, rs.at[n], partner)

    A0 = message(sA0, rA0, a0_s, a0_r, (xp, xm))
    A1 = message(sA1, rA1, a1_s, a1_r, (yp, ym))
    A2 = message(sA2, rA2, a2_s, a2_r, (zp, zm))
    B0 = halves(sB0, rB0, b0_s, b0_r, (xp, xm))
    B1 = halves(sB1, rB1, b1_s, b1_r, (yp, ym))
    B2 = halves(sB2, rB2, b2_s, b2_r, (zp, zm))

    second_rings = (
        (own0, W0, s2A.at[0], r2A.at[0], s2B.at[0], r2B.at[0], zp, zm),
        (own1, W1, s2A.at[1], r2A.at[1], s2B.at[1], r2B.at[1], zp, zm),
        (own2, W2, s2A2, r2A2, s2B2, r2B2, xp, xm),
    )

    def A_second(n, side):
        own, width, sA, rA, sB, rB, plus, minus = second_rings[n]
        return remote(sA.at[side], rA.at[side], p2a_s.at[n], p2a_r.at[n, side], (plus, minus)[side])

    def B_second(n, side, half):
        own, width, sA, rA, sB, rB, plus, minus = second_rings[n]
        return remote(sB.at[side, half], rB.at[side, half], p2b_s.at[n], p2b_r.at[n], (plus, minus)[side])

    def second_phase(n, m, j):
        own, width, sA, rA, sB, rB, plus, minus = second_rings[n]
        chunk = own.at[m]

        @pl.when(j == 0)
        def _():
            for side in range(2):
                encode(chunk, 128 * side, 128, 0, width, sA.at[side])
            for side in range(2):
                A_second(n, side).start()

        for side in range(2):

            @pl.when(j == 1 + side)
            def _():
                encode(chunk, 128 * (1 - side), 128, 0, width, sB.at[side, 1 - side])
                B_second(n, side, 1 - side).start()
                A_second(n, side).wait_recv()
                r = 128 * side
                decode_sum(chunk, r, 0, chunk, r, 0, 128, width, [rA.at[side]])
                encode(chunk, r, 128, 0, width, sB.at[side, side])
                B_second(n, side, side).start()

    dims = (((0,), (0,)), ((), ()))

    def start_group(i):
        j, k = lax.div(i, 4), rem4(i)
        a = acc.at[lax.rem(i, SLOTS)]
        need, have = pick(i, NEED), pick(i, HAVE)
        for t in range(2):

            @pl.when(need > t)
            def _():
                local_tok(have + t).wait()
                remote_tok(have + t).wait_recv()

        x, z = place(k, j)
        x2, z2 = place(j, k)
        cols = pl.ds(row0(x, z), 256)
        cols2 = pl.ds(row0(x2, z2), 256)
        a[:, :C2] = lax.dot_general(
            tok[0, :, cols], w[0, :, :C2], dims, preferred_element_type=jnp.float32
        ) + lax.dot_general(tok[1, :, cols], w[1, :, :C2], dims, preferred_element_type=jnp.float32)
        a[:, C2:] = lax.dot_general(
            tok[0, :, cols2], w[0, :, C2:], dims, preferred_element_type=jnp.float32
        ) + lax.dot_general(tok[1, :, cols2], w[1, :, C2:], dims, preferred_element_type=jnp.float32)
        g = x * 4 + z
        y1, y2, y3 = (pl.multiple_of(rem4(Y + d) * 64, 64) for d in (1, 2, 3))
        encode(a, y2, 32, C1, W1, sA1.at[g, 0])
        encode(a, y2 + 32, 32, C1, W1, sA1.at[g, 1])
        encode(a, y1 + 32, 32, C1, W1, sB1.at[g, 0, 1])
        encode(a, y3, 32, C1, W1, sB1.at[g, 1, 0])
        for side in range(2):
            A1(g, side).start()
        for side in range(2):
            B1(g, side, 1 - side).start()

        @pl.when(k == 0)
        def _():
            for side in range(2):
                encode(a, 128 * side, 128, C0, W0, sA0.at[z, side])
                encode(a, 128 * side, 128, C2, W2, sA2.at[x2, side])
            for side in range(2):
                A0(z, side).start()
                A2(x2, side).start()

        for side in range(2):

            @pl.when(k == 1 + side)
            def _():
                r = 128 * (1 - side)
                encode(a, r, 128, C0, W0, sB0.at[z, side, 1 - side])
                encode(a, r, 128, C2, W2, sB2.at[x2, side, 1 - side])
                B0(z, side, 1 - side).start()
                B2(x2, side, 1 - side).start()

    def send_group(i):
        j, k = lax.div(i, 4), rem4(i)
        a = acc.at[lax.rem(i, SLOTS)]
        x, z = place(k, j)
        x2, z2 = place(j, k)
        g = x * 4 + z
        for side in range(2):
            A1(g, side).wait_recv()
        for side in range(2):
            r = pl.multiple_of(rem4(Y + 1 + 2 * side) * 64, 64) + 32 * side
            decode_sum(a, r, C1, a, r, C1, 32, W1, [rA1.at[g, side]])
            encode(a, r, 32, C1, W1, sB1.at[g, side, side])
        for side in range(2):
            B1(g, side, side).start()
        for side in range(2):

            @pl.when(k == 1 + side)
            def _():
                r = 128 * side
                A0(z, side).wait_recv()
                A2(x2, side).wait_recv()
                decode_sum(a, r, C0, a, r, C0, 128, W0, [rA0.at[z, side]])
                encode(a, r, 128, C0, W0, sB0.at[z, side, side])
                decode_sum(a, r, C2, a, r, C2, 128, W2, [rA2.at[x2, side]])
                encode(a, r, 128, C2, W2, sB2.at[x2, side, side])
                B0(z, side, side).start()
                B2(x2, side, side).start()

    def sum_group(i):
        j, k = lax.div(i, 4), rem4(i)
        a = acc.at[lax.rem(i, SLOTS)]
        x, z = place(k, j)
        x2, z2 = place(j, k)
        g = x * 4 + z
        both(sB1, rB1, b1_s, b1_r, g).wait_recv()
        mine = pl.multiple_of(Y * 64, 64)
        x64 = pl.multiple_of(x * 64, 64)
        for h in range(2):
            decode_sum(
                own1.at[z], x64 + 32 * h, 0, a, mine + 32 * h, C1, 32, W1, [rB1.at[g, 0, h], rB1.at[g, 1, h]]
            )

        @pl.when(k == 3)
        def _():
            both(sB0, rB0, b0_s, b0_r, z).wait_recv()
            for h in range(2):
                r = 128 * h
                decode_sum(own0.at[z], r, 0, a, r, C0, 128, W0, [rB0.at[z, 0, h], rB0.at[z, 1, h]])
            second_phase(0, z, j)
            second_phase(1, z, j)
            both(sB2, rB2, b2_s, b2_r, x2).wait_recv()
            for h in range(2):
                r = 128 * h
                decode_sum(own2.at[x2], r, 0, a, r, C2, 128, W2, [rB2.at[x2, 0, h], rB2.at[x2, 1, h]])
            second_phase(2, x2, j)

    def step(i, carry):
        @pl.when(i < 16)
        def _():
            start_group(i)

        @pl.when((i >= LAG_B) & (i < 16 + LAG_B))
        def _():
            send_group(i - LAG_B)

        @pl.when(i >= LAG_SUM)
        def _():
            sum_group(i - LAG_SUM)

        return carry

    lax.fori_loop(0, 16 + LAG_SUM, step, 0)

    def ring_y(d):
        return dev(X, rem4(Y + d), Z, C)

    def ring_x(d):
        return dev(rem4(X + d), Y, Z, C)

    third_rings = (
        (own0.at[Z], W0, Y, s3.at[0], r3.at[0], ring_y),
        (own1.at[Z], W1, X, s3.at[1], r3.at[1], ring_x),
        (own2.at[X], W2, Y, s32, r32, ring_y),
    )

    def third(n, d):
        own, width, at, S, R, to = third_rings[n]
        return remote(S.at[d - 1], R.at[d - 1], p3_s.at[n], p3_r.at[n], to(d))

    for n, m in ((0, Z), (1, Z), (2, X)):
        own, width, sA, rA, sB, rB, plus, minus = second_rings[n]
        remote(sB, rB, p2b_s.at[n], p2b_r.at[n], partner).wait_recv()
        for h in range(2):
            r = 128 * h
            decode_sum(own.at[m], r, 0, own.at[m], r, 0, 128, width, [rB.at[0, h], rB.at[1, h]])
        own, width, at, S, R, to = third_rings[n]
        for d in (2, 1, 3):
            encode(own, pl.multiple_of(rem4(at + d) * 64, 64), 64, 0, width, S.at[d - 1])
        for d in (2, 1, 3):
            third(n, d).start()
    col = 0
    square = jnp.zeros((8, 128), jnp.float32)
    for n, (own, width, at, S, R, to) in enumerate(third_rings):
        r = pl.multiple_of(at * 64, 64)
        remote(S, R, p3_s.at[n], p3_r.at[n], partner).wait_recv()
        decode_sum(own, r, 0, own, r, 0, 64, width, [R.at[d] for d in range(3)])
        for t in range(8):
            for j in range(width // 128):
                v = own[pl.ds(r + t * 8, 8), pl.ds(j * 128, 128)]
                fin[pl.ds(t * 8, 8), pl.ds(col + j * 128, 128)] = v
                square = square + v * v
        col += width

    nrm1[here] = jnp.sum(square, axis=0, keepdims=True)
    exchange(nrm1, here, 8, near, none_s, none_r)
    theirs = pl.ds(pl.multiple_of((1 - C) * 32, 32), 32)
    mine = pl.ds(pl.multiple_of(C * 32, 32), 32)
    swap = remote(fin.at[theirs], finr, f_s, f_r, partner)
    swap.start()
    everything(nrm1, 8, none_s, none_r).wait_recv()
    nrm2[plane] = total_of(nrm1, 8)
    exchange(nrm2, plane, 16, far, ntwo_s, ntwo_r)

    for S, ss in ((sA0, a0_s), (sB0, b0_s), (sA1, a1_s), (sB1, b1_s), (sA2, a2_s), (sB2, b2_s)):
        remote(S, S, ss, f_r, partner).wait_send()
    for n in range(3):
        own, width, sA, rA, sB, rB, plus, minus = second_rings[n]
        remote(sA, rA, p2a_s.at[n], f_r, partner).wait_send()
        remote(sB, rB, p2b_s.at[n], f_r, partner).wait_send()
        own, width, at, S, R, to = third_rings[n]
        remote(S, R, p3_s.at[n], f_r, partner).wait_send()
    remote(tok_hbm, tok.at[1], tok_s, f_r, partner).wait_send()
    in_cot.wait_send()
    in_idx.wait_send()
    for slots, count, ss in ((cnt1, 8, one_s), (cnt2, 16, two_s), (nrm1, 8, none_s), (nrm2, 16, ntwo_s)):
        everything(slots, count, ss, f_r).wait_send()
    swap.wait()
    everything(nrm2, 16, ntwo_s, ntwo_r).wait_recv()
    square = total_of(nrm2, 16)
    root_mean = jnp.sqrt(jnp.sum(square, keepdims=True) / (D * QW))
    factor = 1.0 / jnp.maximum(root_mean, 1.0)
    grad_ref[:, my_cols] = fin[mine, :] * factor
    grad_ref[:, other_cols] = finr[...] * factor


def shards(tokens_in, query_cotangent, task_index, loss_weights, master, moment_first, moment_second):
    i16 = jnp.int16

    def msgs(lead, rows, width):
        return pltpu.VMEM((*lead, tiles(rows, width) + 1, 16, 128), i16)

    f32 = jnp.float32
    dma = pltpu.SemaphoreType.DMA
    scratch = [
        pltpu.SMEM((TASKS,), jnp.int32),
        pltpu.VMEM((2, TOK, D), jnp.bfloat16),
        pltpu.VMEM((2, TOK, HALF), jnp.bfloat16),
        pltpu.VMEM((2, 8, 128), jnp.int32),
        pltpu.VMEM((2, 8, 128), f32),
        pltpu.VMEM((SLOTS, 256, HALF), f32),
        pltpu.VMEM((4, 256, W0), f32),
        pltpu.VMEM((4, 256, W1), f32),
        pltpu.VMEM((4, 256, W2), f32),
        msgs((4, 2), 128, W0), msgs((4, 2), 128, W0), msgs((4, 2, 2), 128, W0), msgs((4, 2, 2), 128, W0),
        msgs((4, 2), 128, W2), msgs((4, 2), 128, W2), msgs((4, 2, 2), 128, W2), msgs((4, 2, 2), 128, W2),
        msgs((16, 2), 32, W1), msgs((16, 2), 32, W1), msgs((16, 2, 2), 32, W1), msgs((16, 2, 2), 32, W1),
        msgs((2, 2), 128, W0), msgs((2, 2), 128, W0), msgs((2, 2, 2), 128, W0), msgs((2, 2, 2), 128, W0),
        msgs((2,), 128, W2), msgs((2,), 128, W2), msgs((2, 2), 128, W2), msgs((2, 2), 128, W2),
        msgs((2, 3), 64, W0), msgs((2, 3), 64, W0), msgs((3,), 64, W2), msgs((3,), 64, W2),
        pltpu.VMEM((8, 1, 128), jnp.int32),
        pltpu.VMEM((16, 1, 128), jnp.int32),
        pltpu.VMEM((8, 1, 128), f32),
        pltpu.VMEM((16, 1, 128), f32),
        pltpu.VMEM((64, HALF), f32),
        pltpu.VMEM((32, HALF), f32),
        dma((19,)), dma(()), dma((16,)), dma((2,)), dma((2,)),
        dma(()), dma(()), dma(()), dma(()), dma(()), dma(()), dma(()), dma(()),
        dma(()), dma((4, 2)), dma(()), dma((4,)),
        dma(()), dma((16, 2)), dma(()), dma((16,)),
        dma(()), dma((4, 2)), dma(()), dma((4,)),
        dma((3,)), dma((3, 2)), dma((3,)), dma((3,)), dma((3,)), dma((3,)),
        dma(()), dma(()),
    ]
    hbm = pl.BlockSpec(memory_space=pl.ANY)
    vmem = pl.BlockSpec(memory_space=pltpu.VMEM)
    clipped = pl.pallas_call(
        kernel,
        out_shape=jax.ShapeDtypeStruct((32, QW), f32),
        in_specs=[hbm] * 4,
        out_specs=vmem,
        scratch_shapes=scratch,
        compiler_params=pltpu.CompilerParams(
            collective_id=0, has_side_effects=True, vmem_limit_bytes=63 * 1024 * 1024
        ),
    )(tokens_in, query_cotangent, task_index.reshape(8, 128), loss_weights)
    new_first = beta_one * moment_first + (1.0 - beta_one) * clipped
    new_second = beta_two * moment_second + (1.0 - beta_two) * clipped * clipped
    direction = new_first / corr_one / (jnp.sqrt(new_second / corr_two) + adam_eps)
    new_master = master - step_rate * (direction + decay_rate * master)
    return (new_master, new_first, new_second)


def solution(mesh):
    finer = Mesh(mesh.devices.reshape(2, 4, 2, 4, 2), AXES)
    rows = P(AXES, None)
    in_specs = (rows, rows, P(AXES), P(), rows, rows, rows)
    return jax.shard_map(
        shards, mesh=finer, in_specs=in_specs, out_specs=(rows, rows, rows), check_vma=False
    )
```

time: 350 us -> 77.5 us (0.22)
  waiting for transfers between devices: 180 us -> 0 us
  blocking collectives: 100 us -> 0 us
  Pallas kernels: 0 us -> 74.7 us
  matrix products: 26 us -> 0 us
  local copies, waits for them, and re-layouts: 23 us -> 0.01 us
  between operations: 14.8 us -> 0.69 us
    reduce_scatter x1 -> x0, waiting for transfers between devices: 180 us -> none  [shards(): lax.psum_scatter(products.reshape(lax.axis_size(DP) * group_rows, feature...]
    pallas_call x0 -> x1, Pallas kernels: none -> 74.7 us  [shards(): pl.pallas_call(kernel, out_shape=jax.ShapeDtypeStruct((32, QW), f32), in_...]
    psum x10 -> x0, blocking collectives: 66.3 us -> none  [over_axes(): value = lax.psum(value, axis)]
    all_to_all x1 -> x0, blocking collectives: 33.8 us -> none  [summed_on_arrival(): lax.all_to_all(blocks, axis, split_axis=0, concat_axis=0, tiled=True)]
    unnamed x1 -> x0, matrix products: 26 us -> none
    transpose x1 -> x0, local copies, waits for them, and re-layouts: 23 us -> none  [shards(): jnp.einsum('ntdr,nq->dtrq', arranged, weighted, preferred_element_type=jn...]
  transfers between devices with their start and end apart: 1 -> 0, of which waited for: 1 -> 0; matrix products, arithmetic and copies ran while one was open for 0% -> 0% of each run, Pallas kernels for 0% -> 0%
where the time goes in v2:
time: 77.5 us; the launch traced here: 77.3 us
  Pallas kernels  74.7 us (96%)
  other arithmetic  1.94 us (3%)
    pallas_call x1, Pallas kernels, shards(): pl.pallas_call(kernel, out_shape=jax.ShapeDtypeStruct((32, QW), f32), in_...  74.7 us
    sub x1, other arithmetic, shards(): new_master = master - step_rate * (direction + decay_rate * master)  1.94 us

profile of v2, /device:TPU:0, one launch (start us, length us, event | category | flops | bytes accessed | tf_op | source)
XLA Modules:
  0.0 77.3 jit_solution(7981449500752919573)
XLA Ops:
  0.6 0.0 copy-start.2
  0.6 0.0 copy-start.1
  0.7 0.0 copy-start
  0.7 74.7 %shard_map.94 = f32[32,2048]{1,0:T(8,128)} custom-call(bf16[1024,4096]{1,0:T(8,128)(2,1)} %tok_hbm.1, bf16[1024,2048]{1,0:T(8,128)(2,1)} %cot_hbm.1, s32[8,128]{1,0:T(8,128)} %bitcast.1, s32[16]{0:T(128)} %lw_hbm.1), custom_call_target="tpu_custom_call" | custom-call | tf_op jit(solution)/shard_map/pallas_call | solution.py:549
  75.3 0.0 copy-done.2
  75.3 0.0 copy-done.1
  75.4 0.0 copy-done
  75.4 1.9 %multiply_subtract_fusion = (f32[32,2048]{1,0:T(8,128)}, f32[32,2048]{1,0:T(8,128)}, f32[32,2048]{1,0:T(8,128)}) fusion(f32[32,2048]{1,0:T(8,128)S(1)} %copy-done, f32[32,2048]{1,0:T(8,128)} %shard_map.94, f32[32,2048]{1,0:T(8,128)S(1)} %copy-done.1, f32[32,2048]{1,0:T(8,128)S(1)} %copy-done.2), kind=kLoop, calls=%fused_computation.2 | loop fusion | flops 983040 | bytes 1835008 | tf_op jit(solution)/shard_map/sub | solution.py:562
Async XLA Ops:
  0.6 74.7 %copy-start.2 = (f32[32,2048]{1,0:T(8,128)S(1)}, f32[32,2048]{1,0:T(8,128)}, u32[]{:S(2)}) copy-start(f32[32,2048]{1,0:T(8,128)} %param.13) | copy-start | bytes 786436
  0.6 74.7 %copy-start.1 = (f32[32,2048]{1,0:T(8,128)S(1)}, f32[32,2048]{1,0:T(8,128)}, u32[]{:S(2)}) copy-start(f32[32,2048]{1,0:T(8,128)} %param.12) | copy-start | bytes 786436
  0.7 74.7 %copy-start = (f32[32,2048]{1,0:T(8,128)S(1)}, f32[32,2048]{1,0:T(8,128)}, u32[]{:S(2)}) copy-start(f32[32,2048]{1,0:T(8,128)} %param.11) | copy-start | bytes 786436

commit v3 on v2

--- a/solution.py
+++ b/solution.py
@@ -47,49 +47,52 @@
     return (rows // 16) * (width // 128)
 
 
-def encode(src, r0, rows, c0, width, msg):
+def encode(src, starts, rows, c0, width, msg):
     nc = width // 128
-    unroll = min(8, rows // 16)
-
-    def largest(t, ms):
-        out = []
-        for j in range(nc):
-            a = jnp.abs(src[pl.ds(r0 + t * 16, 16), pl.ds(c0 + j * 128, 128)])
-            out.append(jnp.maximum(ms[2 * j], a[:8]))
-            out.append(jnp.maximum(ms[2 * j + 1], a[8:]))
-        return tuple(out)
-
-    zero = jnp.zeros((8, 128), jnp.float32)
-    ms = lax.fori_loop(0, rows // 16, largest, (zero,) * (2 * nc), unroll=unroll)
+    steps = rows // 16
+    unroll = min(8, steps)
+    ms = (jnp.zeros((8, 128), jnp.float32),) * (2 * nc)
+    for r0 in starts:
+
+        def largest(t, ms):
+            out = []
+            for j in range(nc):
+                a = jnp.abs(src[pl.ds(r0 + t * 16, 16), pl.ds(c0 + j * 128, 128)])
+                out.append(jnp.maximum(ms[2 * j], a[:8]))
+                out.append(jnp.maximum(ms[2 * j + 1], a[8:]))
+            return tuple(out)
+
+        ms = lax.fori_loop(0, steps, largest, ms, unroll=unroll)
     m = ms[0]
     for other in ms[1:]:
         m = jnp.maximum(m, other)
     e = jnp.ceil(jnp.log2(jnp.maximum(m, 1e-30)) + 0.001)
     inv = jnp.exp2(-e) * TOP
     inv = jnp.concatenate([inv, inv], axis=0)
-
-    def put(t, carry):
-        for j in range(nc):
-            v = src[pl.ds(r0 + t * 16, 16), pl.ds(c0 + j * 128, 128)]
-            msg[t * nc + j] = jnp.round(v * inv).astype(jnp.int32).astype(jnp.int16)
-        return carry
-
-    lax.fori_loop(0, rows // 16, put, 0, unroll=unroll)
-    msg[tiles(rows, width)] = jnp.concatenate([e, e], axis=0).astype(jnp.int32).astype(jnp.int16)
+    for n, r0 in enumerate(starts):
+
+        def put(t, carry):
+            for j in range(nc):
+                v = src[pl.ds(r0 + t * 16, 16), pl.ds(c0 + j * 128, 128)]
+                msg[(n * steps + t) * nc + j] = jnp.round(v * inv).astype(jnp.int32).astype(jnp.int16)
+            return carry
+
+        lax.fori_loop(0, steps, put, 0, unroll=unroll)
+    msg[msg.shape[0] - 1] = jnp.concatenate([e, e], axis=0).astype(jnp.int32).astype(jnp.int16)
 
 
 def decode_sum(dst, dr0, dc0, src, sr0, sc0, rows, width, msgs):
     nc = width // 128
     scales = []
-    for msg in msgs:
-        e = msg[tiles(rows, width)].astype(jnp.int32).astype(jnp.float32)
+    for msg, _ in msgs:
+        e = msg[msg.shape[0] - 1].astype(jnp.int32).astype(jnp.float32)
         scales.append(jnp.exp2(e) * (1.0 / TOP))
 
     def add(t, carry):
         for j in range(nc):
             v = src[pl.ds(sr0 + t * 16, 16), pl.ds(sc0 + j * 128, 128)]
-            for msg, scale in zip(msgs, scales):
-                v = v + msg[t * nc + j].astype(jnp.int32).astype(jnp.float32) * scale
+            for (msg, first), scale in zip(msgs, scales):
+                v = v + msg[first + t * nc + j].astype(jnp.int32).astype(jnp.float32) * scale
             dst[pl.ds(dr0 + t * 16, 16), pl.ds(dc0 + j * 128, 128)] = v
         return carry
 
@@ -112,14 +115,19 @@
     p2a_s, p2a_r, p2b_s, p2b_r, p3_s, p3_r, f_s, f_r,
 ):
     xh = lax.axis_index("task_0")
-    Z = lax.axis_index("task_1")
+    zz = lax.axis_index("task_1")
     xl = lax.axis_index("dp_0")
     Y = lax.axis_index("dp_1")
     C = lax.axis_index("dp_2")
-    X = xh * 2 + xl
+    xx = xh * 2 + xl
+    X = jnp.where(C == 0, xx, zz)
+    Z = jnp.where(C == 0, zz, xx)
+
+    def chip(x, y, z, c):
+        return (lax.div(x, 2), z, lax.rem(x, 2), y, c)
 
     def dev(x, y, z, c):
-        return (lax.div(x, 2), z, lax.rem(x, 2), y, c)
+        return chip(jnp.where(C == 0, x, z), y, jnp.where(C == 0, z, x), c)
 
     def rem4(v):
         return lax.rem(v, 4)
@@ -128,23 +136,26 @@
     xp, xm = dev(rem4(X + 1), Y, Z, C), dev(rem4(X + 3), Y, Z, C)
     yp, ym = dev(X, rem4(Y + 1), Z, C), dev(X, rem4(Y + 3), Z, C)
     zp, zm = dev(X, Y, rem4(Z + 1), C), dev(X, Y, rem4(Z + 3), C)
-    partner = dev(X, Y, Z, 1 - C)
+    partner = chip(xx, Y, zz, 1 - C)
 
     def near(k):
         p = lax.rem(Y * 2 + C + k, 8)
-        return dev(X, lax.div(p, 2), Z, lax.rem(p, 2))
+        return chip(xx, lax.div(p, 2), zz, lax.rem(p, 2))
 
     def far(k):
-        p = lax.rem(X * 4 + Z + k, 16)
-        return dev(lax.div(p, 4), Y, lax.rem(p, 4), C)
+        p = lax.rem(xx * 4 + zz + k, 16)
+        return chip(lax.div(p, 4), Y, lax.rem(p, 4), C)
 
     def remote(src, dst, ssem, rsem, to):
         return pltpu.make_async_remote_copy(
             src_ref=src, dst_ref=dst, send_sem=ssem, recv_sem=rsem, device_id=to, device_id_type=MESH
         )
 
+    def chip_row0(x, z):
+        return pl.multiple_of(lax.div(x, 2) * 2048 + z * 512 + lax.rem(x, 2) * 256, 256)
+
     def row0(x, z):
-        return pl.multiple_of(lax.div(x, 2) * 2048 + z * 512 + lax.rem(x, 2) * 256, 256)
+        return chip_row0(jnp.where(C == 0, x, z), jnp.where(C == 0, z, x))
 
     def place(p, q):
         return rem4(X + pick(p, ORDER)), rem4(Z + pick(q, ORDER))
@@ -170,8 +181,9 @@
         return pltpu.make_async_copy(tok_hbm.at[:, cols], tok.at[0, :, cols], loc_sem.at[3 + i])
 
     def remote_tok(i):
-        x, z = place(pick(i, FETCH_X), pick(i, FETCH_Z))
-        cols = pl.ds(row0(x, z), 256)
+        p, q = pick(i, FETCH_X), pick(i, FETCH_Z)
+        p, q = jnp.where(C == 0, q, p), jnp.where(C == 0, p, q)
+        cols = pl.ds(chip_row0(rem4(xx + pick(p, ORDER)), rem4(zz + pick(q, ORDER))), 256)
         return remote(tok_hbm.at[:, cols], tok.at[1, :, cols], tok_s, tok_r.at[i], partner)
 
     cp_idx.wait()
@@ -210,12 +222,13 @@
         remote_tok(i).start()
         return carry
 
-    lax.fori_loop(0, 16, start_tok, 0)
+    lax.fori_loop(0, 5, start_tok, 0)
 
     everything(cnt1, 8, one_s, one_r).wait_recv()
-    plane = X * 4 + Z
+    plane = xx * 4 + zz
     cnt2[plane] = total_of(cnt1, 8)
     exchange(cnt2, plane, 16, far, two_s, two_r)
+    lax.fori_loop(5, 16, start_tok, 0)
     everything(cnt2, 16, two_s, two_r).wait_recv()
     counts = jnp.broadcast_to(total_of(cnt2, 16), (TASKS, 128))
     diagonal = lax.broadcasted_iota(jnp.int32, (TASKS, 128), 0) == lax.broadcasted_iota(
@@ -251,7 +264,8 @@
 
     def message(S, R, ss, rs, ways):
         def at(n, side):
-            return remote(S.at[n, side], R.at[n, side], ss, rs.at[n, side], ways[side])
+            sem = rs.at[n, side] if len(rs.shape) == 2 else rs.at[n]
+            return remote(S.at[n, side], R.at[n, side], ss, sem, ways[side])
 
         return at
 
@@ -266,9 +280,9 @@
 
     A0 = message(sA0, rA0, a0_s, a0_r, (xp, xm))
     A1 = message(sA1, rA1, a1_s, a1_r, (yp, ym))
+    B1 = message(sB1, rB1, b1_s, b1_r, (yp, ym))
     A2 = message(sA2, rA2, a2_s, a2_r, (zp, zm))
     B0 = halves(sB0, rB0, b0_s, b0_r, (xp, xm))
-    B1 = halves(sB1, rB1, b1_s, b1_r, (yp, ym))
     B2 = halves(sB2, rB2, b2_s, b2_r, (zp, zm))
 
     second_rings = (
@@ -292,7 +306,7 @@
         @pl.when(j == 0)
         def _():
             for side in range(2):
-                encode(chunk, 128 * side, 128, 0, width, sA.at[side])
+                encode(chunk, (128 * side,), 128, 0, width, sA.at[side])
             for side in range(2):
                 A_second(n, side).start()
 
@@ -300,12 +314,12 @@
 
             @pl.when(j == 1 + side)
             def _():
-                encode(chunk, 128 * (1 - side), 128, 0, width, sB.at[side, 1 - side])
+                encode(chunk, (128 * (1 - side),), 128, 0, width, sB.at[side, 1 - side])
                 B_second(n, side, 1 - side).start()
                 A_second(n, side).wait_recv()
                 r = 128 * side
-                decode_sum(chunk, r, 0, chunk, r, 0, 128, width, [rA.at[side]])
-                encode(chunk, r, 128, 0, width, sB.at[side, side])
+                decode_sum(chunk, r, 0, chunk, r, 0, 128, width, [(rA.at[side], 0)])
+                encode(chunk, (r,), 128, 0, width, sB.at[side, side])
                 B_second(n, side, side).start()
 
     dims = (((0,), (0,)), ((), ()))
@@ -333,20 +347,16 @@
         ) + lax.dot_general(tok[1, :, cols2], w[1, :, C2:], dims, preferred_element_type=jnp.float32)
         g = x * 4 + z
         y1, y2, y3 = (pl.multiple_of(rem4(Y + d) * 64, 64) for d in (1, 2, 3))
-        encode(a, y2, 32, C1, W1, sA1.at[g, 0])
-        encode(a, y2 + 32, 32, C1, W1, sA1.at[g, 1])
-        encode(a, y1 + 32, 32, C1, W1, sB1.at[g, 0, 1])
-        encode(a, y3, 32, C1, W1, sB1.at[g, 1, 0])
+        encode(a, (y2, y1 + 32), 32, C1, W1, sA1.at[g, 0])
+        encode(a, (y2 + 32, y3), 32, C1, W1, sA1.at[g, 1])
         for side in range(2):
             A1(g, side).start()
-        for side in range(2):
-            B1(g, side, 1 - side).start()
 
         @pl.when(k == 0)
         def _():
             for side in range(2):
-                encode(a, 128 * side, 128, C0, W0, sA0.at[z, side])
-                encode(a, 128 * side, 128, C2, W2, sA2.at[x2, side])
+                encode(a, (128 * side,), 128, C0, W0, sA0.at[z, side])
+                encode(a, (128 * side,), 128, C2, W2, sA2.at[x2, side])
             for side in range(2):
                 A0(z, side).start()
                 A2(x2, side).start()
@@ -356,8 +366,8 @@
             @pl.when(k == 1 + side)
             def _():
                 r = 128 * (1 - side)
-                encode(a, r, 128, C0, W0, sB0.at[z, side, 1 - side])
-                encode(a, r, 128, C2, W2, sB2.at[x2, side, 1 - side])
+                encode(a, (r,), 128, C0, W0, sB0.at[z, side, 1 - side])
+                encode(a, (r,), 128, C2, W2, sB2.at[x2, side, 1 - side])
                 B0(z, side, 1 - side).start()
                 B2(x2, side, 1 - side).start()
 
@@ -371,10 +381,10 @@
             A1(g, side).wait_recv()
         for side in range(2):
             r = pl.multiple_of(rem4(Y + 1 + 2 * side) * 64, 64) + 32 * side
-            decode_sum(a, r, C1, a, r, C1, 32, W1, [rA1.at[g, side]])
-            encode(a, r, 32, C1, W1, sB1.at[g, side, side])
-        for side in range(2):
-            B1(g, side, side).start()
+            decode_sum(a, r, C1, a, r, C1, 32, W1, [(rA1.at[g, side], 0)])
+            encode(a, (r,), 32, C1, W1, sB1.at[g, side])
+        for side in range(2):
+            B1(g, side).start()
         for side in range(2):
 
             @pl.when(k == 1 + side)
@@ -382,10 +392,10 @@
                 r = 128 * side
                 A0(z, side).wait_recv()
                 A2(x2, side).wait_recv()
-                decode_sum(a, r, C0, a, r, C0, 128, W0, [rA0.at[z, side]])
-                encode(a, r, 128, C0, W0, sB0.at[z, side, side])
-                decode_sum(a, r, C2, a, r, C2, 128, W2, [rA2.at[x2, side]])
-                encode(a, r, 128, C2, W2, sB2.at[x2, side, side])
+                decode_sum(a, r, C0, a, r, C0, 128, W0, [(rA0.at[z, side], 0)])
+                encode(a, (r,), 128, C0, W0, sB0.at[z, side, side])
+                decode_sum(a, r, C2, a, r, C2, 128, W2, [(rA2.at[x2, side], 0)])
+                encode(a, (r,), 128, C2, W2, sB2.at[x2, side, side])
                 B0(z, side, side).start()
                 B2(x2, side, side).start()
 
@@ -399,22 +409,21 @@
         mine = pl.multiple_of(Y * 64, 64)
         x64 = pl.multiple_of(x * 64, 64)
         for h in range(2):
-            decode_sum(
-                own1.at[z], x64 + 32 * h, 0, a, mine + 32 * h, C1, 32, W1, [rB1.at[g, 0, h], rB1.at[g, 1, h]]
-            )
+            parts = [(rB1.at[g, h], 0), (rA1.at[g, 1 - h], tiles(32, W1))]
+            decode_sum(own1.at[z], x64 + 32 * h, 0, a, mine + 32 * h, C1, 32, W1, parts)
 
         @pl.when(k == 3)
         def _():
             both(sB0, rB0, b0_s, b0_r, z).wait_recv()
             for h in range(2):
                 r = 128 * h
-                decode_sum(own0.at[z], r, 0, a, r, C0, 128, W0, [rB0.at[z, 0, h], rB0.at[z, 1, h]])
+                decode_sum(own0.at[z], r, 0, a, r, C0, 128, W0, [(rB0.at[z, 0, h], 0), (rB0.at[z, 1, h], 0)])
             second_phase(0, z, j)
             second_phase(1, z, j)
             both(sB2, rB2, b2_s, b2_r, x2).wait_recv()
             for h in range(2):
                 r = 128 * h
-                decode_sum(own2.at[x2], r, 0, a, r, C2, 128, W2, [rB2.at[x2, 0, h], rB2.at[x2, 1, h]])
+                decode_sum(own2.at[x2], r, 0, a, r, C2, 128, W2, [(rB2.at[x2, 0, h], 0), (rB2.at[x2, 1, h], 0)])
             second_phase(2, x2, j)
 
     def step(i, carry):
@@ -455,10 +464,10 @@
         remote(sB, rB, p2b_s.at[n], p2b_r.at[n], partner).wait_recv()
         for h in range(2):
             r = 128 * h
-            decode_sum(own.at[m], r, 0, own.at[m], r, 0, 128, width, [rB.at[0, h], rB.at[1, h]])
+            decode_sum(own.at[m], r, 0, own.at[m], r, 0, 128, width, [(rB.at[0, h], 0), (rB.at[1, h], 0)])
         own, width, at, S, R, to = third_rings[n]
         for d in (2, 1, 3):
-            encode(own, pl.multiple_of(rem4(at + d) * 64, 64), 64, 0, width, S.at[d - 1])
+            encode(own, (pl.multiple_of(rem4(at + d) * 64, 64),), 64, 0, width, S.at[d - 1])
         for d in (2, 1, 3):
             third(n, d).start()
     col = 0
@@ -466,7 +475,7 @@
     for n, (own, width, at, S, R, to) in enumerate(third_rings):
         r = pl.multiple_of(at * 64, 64)
         remote(S, R, p3_s.at[n], p3_r.at[n], partner).wait_recv()
-        decode_sum(own, r, 0, own, r, 0, 64, width, [R.at[d] for d in range(3)])
+        decode_sum(own, r, 0, own, r, 0, 64, width, [(R.at[d], 0) for d in range(3)])
         for t in range(8):
             for j in range(width // 128):
                 v = own[pl.ds(r + t * 8, 8), pl.ds(j * 128, 128)]
@@ -526,7 +535,7 @@
         pltpu.VMEM((4, 256, W2), f32),
         msgs((4, 2), 128, W0), msgs((4, 2), 128, W0), msgs((4, 2, 2), 128, W0), msgs((4, 2, 2), 128, W0),
         msgs((4, 2), 128, W2), msgs((4, 2), 128, W2), msgs((4, 2, 2), 128, W2), msgs((4, 2, 2), 128, W2),
-        msgs((16, 2), 32, W1), msgs((16, 2), 32, W1), msgs((16, 2, 2), 32, W1), msgs((16, 2, 2), 32, W1),
+        msgs((16, 2), 64, W1), msgs((16, 2), 64, W1), msgs((16, 2), 32, W1), msgs((16, 2), 32, W1),
         msgs((2, 2), 128, W0), msgs((2, 2), 128, W0), msgs((2, 2, 2), 128, W0), msgs((2, 2, 2), 128, W0),
         msgs((2,), 128, W2), msgs((2,), 128, W2), msgs((2, 2), 128, W2), msgs((2, 2), 128, W2),
         msgs((2, 3), 64, W0), msgs((2, 3), 64, W0), msgs((3,), 64, W2), msgs((3,), 64, W2),

time: 77.5 us -> 74.9 us (0.966)
  Pallas kernels: 74.7 us -> 72.1 us
    pallas_call x1, Pallas kernels: 74.7 us -> 72.1 us  [shards(): pl.pallas_call(kernel, out_shape=jax.ShapeDtypeStruct((32, QW), f32), in_...]
where the time goes in v3:
time: 74.9 us; the launch traced here: 74.8 us
  Pallas kernels  72.1 us (96%)
  other arithmetic  1.94 us (3%)
    pallas_call x1, Pallas kernels, shards(): pl.pallas_call(kernel, out_shape=jax.ShapeDtypeStruct((32, QW), f32), in_...  72.1 us
    sub x1, other arithmetic, shards(): new_master = master - step_rate * (direction + decay_rate * master)  1.94 us

profile of v3, /device:TPU:0, one launch (start us, length us, event | category | flops | bytes accessed | tf_op | source)
XLA Modules:
  0.0 74.8 jit_solution(11688002395010767877)
XLA Ops:
  0.6 0.0 copy-start.2
  0.6 0.0 copy-start.1
  0.7 0.0 copy-start
  0.7 72.1 %shard_map.94 = f32[32,2048]{1,0:T(8,128)} custom-call(bf16[1024,4096]{1,0:T(8,128)(2,1)} %tok_hbm.1, bf16[1024,2048]{1,0:T(8,128)(2,1)} %cot_hbm.1, s32[8,128]{1,0:T(8,128)} %bitcast.1, s32[16]{0:T(128)} %lw_hbm.1), custom_call_target="tpu_custom_call" | custom-call | tf_op jit(solution)/shard_map/pallas_call | solution.py:558
  72.8 0.0 copy-done.2
  72.8 0.0 copy-done.1
  72.8 0.0 copy-done
  72.8 1.9 %multiply_subtract_fusion = (f32[32,2048]{1,0:T(8,128)}, f32[32,2048]{1,0:T(8,128)}, f32[32,2048]{1,0:T(8,128)}) fusion(f32[32,2048]{1,0:T(8,128)S(1)} %copy-done, f32[32,2048]{1,0:T(8,128)} %shard_map.94, f32[32,2048]{1,0:T(8,128)S(1)} %copy-done.1, f32[32,2048]{1,0:T(8,128)S(1)} %copy-done.2), kind=kLoop, calls=%fused_computation.2 | loop fusion | flops 983040 | bytes 1835008 | tf_op jit(solution)/shard_map/sub | solution.py:571
Async XLA Ops:
  0.6 72.2 %copy-start.2 = (f32[32,2048]{1,0:T(8,128)S(1)}, f32[32,2048]{1,0:T(8,128)}, u32[]{:S(2)}) copy-start(f32[32,2048]{1,0:T(8,128)} %param.13) | copy-start | bytes 786436
  0.6 72.2 %copy-start.1 = (f32[32,2048]{1,0:T(8,128)S(1)}, f32[32,2048]{1,0:T(8,128)}, u32[]{:S(2)}) copy-start(f32[32,2048]{1,0:T(8,128)} %param.12) | copy-start | bytes 786436
  0.7 72.2 %copy-start = (f32[32,2048]{1,0:T(8,128)S(1)}, f32[32,2048]{1,0:T(8,128)}, u32[]{:S(2)}) copy-start(f32[32,2048]{1,0:T(8,128)} %param.11) | copy-start | bytes 786436

commit v4 on v3

--- a/solution.py
+++ b/solution.py
@@ -260,7 +260,7 @@
                 w[s, rows, cols] = (w[s, rows, cols].astype(jnp.float32) * mat).astype(jnp.bfloat16)
             return carry
 
-        lax.fori_loop(0, 8, weigh, 0)
+        lax.fori_loop(0, 8, weigh, 0, unroll=4)
 
     def message(S, R, ss, rs, ways):
         def at(n, side):
@@ -562,7 +562,7 @@
         out_specs=vmem,
         scratch_shapes=scratch,
         compiler_params=pltpu.CompilerParams(
-            collective_id=0, has_side_effects=True, vmem_limit_bytes=63 * 1024 * 1024
+            collective_id=0, has_side_effects=True, vmem_limit_bytes=62 * 1024 * 1024
         ),
     )(tokens_in, query_cotangent, task_index.reshape(8, 128), loss_weights)
     new_first = beta_one * moment_first + (1.0 - beta_one) * clipped

time: 74.9 us -> 74.4 us (level)
  no operation moved by 1% of the time
where the time goes in v4:
time: 74.4 us; the launch traced here: 74.2 us
  Pallas kernels  71.6 us (96%)
  other arithmetic  1.94 us (3%)
    pallas_call x1, Pallas kernels, shards(): pl.pallas_call(kernel, out_shape=jax.ShapeDtypeStruct((32, QW), f32), in_...  71.6 us
    sub x1, other arithmetic, shards(): new_master = master - step_rate * (direction + decay_rate * master)  1.94 us

profile of v4, /device:TPU:0, one launch (start us, length us, event | category | flops | bytes accessed | tf_op | source)
XLA Modules:
  0.0 74.2 jit_solution(3056871995014560914)
XLA Ops:
  0.6 0.0 copy-start.2
  0.6 0.0 copy-start.1
  0.7 0.0 copy-start
  0.7 71.6 %shard_map.94 = f32[32,2048]{1,0:T(8,128)} custom-call(bf16[1024,4096]{1,0:T(8,128)(2,1)} %tok_hbm.1, bf16[1024,2048]{1,0:T(8,128)(2,1)} %cot_hbm.1, s32[8,128]{1,0:T(8,128)} %bitcast.1, s32[16]{0:T(128)} %lw_hbm.1), custom_call_target="tpu_custom_call" | custom-call | tf_op jit(solution)/shard_map/pallas_call | solution.py:558
  72.2 0.0 copy-done.2
  72.2 0.0 copy-done.1
  72.2 0.0 copy-done
  72.3 1.9 %multiply_subtract_fusion = (f32[32,2048]{1,0:T(8,128)}, f32[32,2048]{1,0:T(8,128)}, f32[32,2048]{1,0:T(8,128)}) fusion(f32[32,2048]{1,0:T(8,128)S(1)} %copy-done, f32[32,2048]{1,0:T(8,128)} %shard_map.94, f32[32,2048]{1,0:T(8,128)S(1)} %copy-done.1, f32[32,2048]{1,0:T(8,128)S(1)} %copy-done.2), kind=kLoop, calls=%fused_computation.2 | loop fusion | flops 983040 | bytes 1835008 | tf_op jit(solution)/shard_map/sub | solution.py:571
Async XLA Ops:
  0.6 71.6 %copy-start.2 = (f32[32,2048]{1,0:T(8,128)S(1)}, f32[32,2048]{1,0:T(8,128)}, u32[]{:S(2)}) copy-start(f32[32,2048]{1,0:T(8,128)} %param.13) | copy-start | bytes 786436
  0.6 71.6 %copy-start.1 = (f32[32,2048]{1,0:T(8,128)S(1)}, f32[32,2048]{1,0:T(8,128)}, u32[]{:S(2)}) copy-start(f32[32,2048]{1,0:T(8,128)} %param.12) | copy-start | bytes 786436
  0.7 71.6 %copy-start = (f32[32,2048]{1,0:T(8,128)S(1)}, f32[32,2048]{1,0:T(8,128)}, u32[]{:S(2)}) copy-start(f32[32,2048]{1,0:T(8,128)} %param.11) | copy-start | bytes 786436
